TPU v7x, 32 devices: a whole 2x2x4 slice. The times are simulated.
32 devices in a mesh: row: 8 (over z, x), col: 4 (over y, core).
Axes of the slice: x: 2, y: 2, z: 4, core: 2. Of those that a mesh axis runs over, the one named last changes fastest.
Arguments:
- tokens: bfloat16 [64, 12288], P('row', 'col'), may hold values from -6 to 6
- past_tokens: bfloat16 [64, 12288], P('row', 'col'), may hold values from -6 to 6
- out_grad: bfloat16 [64, 12288], P('row', 'col'), may hold values from -3 to 3
- w_in: bfloat16 [12288, 24576], P('col', 'row'), may hold values from -0.0546875 to 0.0546875
- w_out: bfloat16 [24576, 12288], P('row', 'col'), may hold values from -0.0390625 to 0.0390625
Outputs:
- layer_out: bfloat16 [64, 12288], P('row', 'col')
- input_grad: bfloat16 [64, 12288], P('row', 'col')
- grad_w_in: bfloat16 [12288, 24576], P('col', 'row')
- grad_w_out: bfloat16 [24576, 12288], P('row', 'col')
All inputs are finite; a program needn't handle non-finite values.
Results may differ from a plain program's by a relative error of at most 0.005.
Values may be sent and summed in bfloat16 or wider, within the bound.
No kernel may reach another device: no remote copies, remote signals or barrier semaphores. Data moves between devices by JAX's collectives and lax.ppermute only.
A program may use at most 128 MiB of HBM per device.

v0:
```python
import jax
import jax.numpy as jnp
from jax import lax
from jax.sharding import PartitionSpec as P


def gelu_parts(pre):
    cdf = 0.5 * (1.0 + jax.scipy.special.erf(pre * 0.7071067811865476))
    slope = cdf + pre * jnp.exp(-0.5 * pre * pre) * 0.3989422804014327
    return (pre * cdf, slope)


def local(tokens, past_tokens, out_grad, w_in, w_out):
    pre_part = jnp.dot(
        lax.all_gather(tokens, "row", axis=0, tiled=True), w_in, preferred_element_type=jnp.float32
    )
    pre_share = lax.psum_scatter(pre_part, "col", scatter_dimension=0, tiled=True)
    hidden_share = gelu_parts(pre_share)[0].astype(jnp.bfloat16)
    hidden_all = lax.all_gather(hidden_share, "col", axis=0, tiled=True)
    block = hidden_all
    layer_out = lax.psum_scatter(
        jnp.dot(block, w_out, preferred_element_type=jnp.float32),
        "row",
        scatter_dimension=0,
        tiled=True,
    ).astype(jnp.bfloat16)
    past_all, grad_all = (
        lax.all_gather(past_tokens, "row", axis=0, tiled=True),
        lax.all_gather(out_grad, "row", axis=0, tiled=True),
    )
    past_part = jnp.dot(past_all, w_in, preferred_element_type=jnp.float32)
    back_part = lax.dot_general(
        grad_all, w_out, (((1,), (1,)), ((), ())), preferred_element_type=jnp.float32
    )
    past_share, back_share = (
        lax.psum_scatter(past_part, "col", scatter_dimension=0, tiled=True),
        lax.psum_scatter(back_part, "col", scatter_dimension=0, tiled=True),
    )
    act_share, slope = gelu_parts(past_share)
    act_local = act_share.astype(jnp.bfloat16)
    grad_local = (back_share * slope).astype(jnp.bfloat16)
    act_all, hidden_grad = (
        lax.all_gather(act_local, "col", axis=0, tiled=True),
        lax.all_gather(grad_local, "col", axis=0, tiled=True),
    )
    grad_w_out = lax.dot_general(
        act_all, grad_all, (((0,), (0,)), ((), ())), preferred_element_type=jnp.float32
    ).astype(jnp.bfloat16)
    grad_w_in = lax.dot_general(
        past_all, hidden_grad, (((0,), (0,)), ((), ())), preferred_element_type=jnp.float32
    ).astype(jnp.bfloat16)
    block = hidden_grad
    input_grad = lax.psum_scatter(
        lax.dot_general(block, w_in, (((1,), (1,)), ((), ())), preferred_element_type=jnp.float32),
        "row",
        scatter_dimension=0,
        tiled=True,
    ).astype(jnp.bfloat16)
    return (layer_out, input_grad, grad_w_in, grad_w_out)


def solution(mesh):
    in_specs = (P("row", "col"), P("row", "col"), P("row", "col"), P("col", "row"), P("row", "col"))
    out_specs = (P("row", "col"), P("row", "col"), P("col", "row"), P("row", "col"))
    return jax.shard_map(local, mesh=mesh, in_specs=in_specs, out_specs=out_specs, check_vma=False)
```

profile of v0, /device:TPU:0, one launch (start us, length us, event | category | flops | bytes accessed | tf_op | source)
XLA Modules:
  0.0 301.0 jit_solution(17160969050519650466)
XLA Ops:
  7.2 0.0 copy-start
  7.2 0.0 reduce-scatter.6.cloned.1.call-start
  7.2 33.0 %all_gather.18 = bf16[64,3072]{1,0:T(8,128)(2,1)S(1)} all-gather(bf16[8,3072]{1,0:T(8,128)(2,1)} %param.5), channel_id=1, replica_groups=mesh['row'=8,'col'=4] {'row'}, dimensions={0}, use_global_device_ids=true | all-gather | bytes 442368 | tf_op jit(solution)/shard_map/all_gather | solution.py:15
  40.2 0.0 copy-start.1
  40.2 10.6 %fusion.6 = f32[64,3072]{1,0:T(8,128)} fusion(bf16[64,3072]{1,0:T(8,128)(2,1)S(1)} %all_gather.18, bf16[3072,3072]{1,0:T(8,128)(2,1)} %param.8), kind=kOutput, calls=%fused_computation.12 | convolution fusion | flops 1207959552 | bytes 20054016 | tf_op jit(solution)/shard_map/dot_general | solution.py:14
  50.8 0.0 reduce-scatter.6.cloned.1.call-update
  50.9 0.0 reduce-scatter.10.cloned.1.call-start
  50.9 0.0 copy-done
  50.9 31.0 %all_gather.20 = bf16[64,3072]{1,0:T(8,128)(2,1)S(1)} all-gather(bf16[8,3072]{1,0:T(8,128)(2,1)S(1)} %copy-done), channel_id=1, replica_groups=mesh['row'=8,'col'=4] {'row'}, dimensions={0}, use_global_device_ids=true | all-gather | bytes 442368 | tf_op jit(solution)/shard_map/all_gather | solution.py:29
  81.9 13.1 %fusion.8 = f32[64,3072]{1,0:T(8,128)} fusion(bf16[64,3072]{1,0:T(8,128)(2,1)S(1)} %all_gather.20, bf16[3072,3072]{1,0:T(8,128)(2,1)} %param.9), kind=kOutput, calls=%fused_computation.14 | convolution fusion | flops 1207959552 | bytes 20054016 | tf_op jit(solution)/shard_map/dot_general | solution.py:32
  95.0 0.0 reduce-scatter.10.cloned.1.call-update
  95.0 0.0 reduce-scatter.12.cloned.1.call-start
  95.0 0.0 copy-done.1
  95.0 31.0 %all_gather.21 = bf16[64,3072]{1,0:T(8,128)(2,1)S(1)} all-gather(bf16[8,3072]{1,0:T(8,128)(2,1)S(1)} %copy-done.1), channel_id=1, replica_groups=mesh['row'=8,'col'=4] {'row'}, dimensions={0}, use_global_device_ids=true | all-gather | bytes 442368 | tf_op jit(solution)/shard_map/all_gather | solution.py:28
  126.0 10.6 %fusion.9 = f32[64,3072]{1,0:T(8,128)} fusion(bf16[64,3072]{1,0:T(8,128)(2,1)S(1)} %all_gather.21, bf16[3072,3072]{1,0:T(8,128)(2,1)} %param.8), kind=kOutput, calls=%fused_computation.15 | convolution fusion | flops 1207959552 | bytes 20054016 | tf_op jit(solution)/shard_map/dot_general | solution.py:31
  136.6 0.0 reduce-scatter.12.cloned.1.call-update
  136.7 0.0 reduce-scatter.8.cloned.1.call-start
  136.7 0.0 reduce-scatter.6.cloned.1.call-done
  136.7 1.0 multiply_convert_fusion.1
  137.7 6.7 %all_gather.19 = bf16[64,3072]{1,0:T(8,128)(2,1)S(1)} all-gather(bf16[16,3072]{1,0:T(8,128)(2,1)S(1)} %multiply_convert_fusion.1), channel_id=1, replica_groups=mesh['row'=8,'col'=4] {'col'}, dimensions={0}, use_global_device_ids=true | all-gather | bytes 491520 | tf_op jit(solution)/shard_map/all_gather | solution.py:19
  144.4 10.8 %fusion.7 = f32[64,3072]{1,0:T(8,128)} fusion(bf16[64,3072]{1,0:T(8,128)(2,1)S(1)} %all_gather.19, bf16[3072,3072]{1,0:T(8,128)(2,1)} %param.9), kind=kOutput, calls=%fused_computation.13 | convolution fusion | flops 1207959552 | bytes 20054016 | tf_op jit(solution)/shard_map/dot_general | solution.py:22
  155.2 0.0 reduce-scatter.8.cloned.1.call-update
  155.2 0.0 reduce-scatter.14.cloned.1.call-start
  155.3 0.0 reduce-scatter.10.cloned.1.call-done
  155.3 5.8 %reduce-scatter.12.cloned.1.call-done = f32[16,3072]{1,0:T(8,128)} async-done(((f32[64,3072]{1,0:T(8,128)}), f32[16,3072]{1,0:T(8,128)}) %reduce-scatter.12.cloned.1.call-update) | async-done | bytes 196624 | tf_op jit(solution)/shard_map/reduce_scatter | solution.py:36
  161.1 1.1 multiply_convert_fusion
  162.2 6.1 %all_gather.22 = bf16[64,3072]{1,0:T(8,128)(2,1)S(1)} all-gather(bf16[16,3072]{1,0:T(8,128)(2,1)S(1)} %get-tuple-element.9), channel_id=1, replica_groups=mesh['row'=8,'col'=4] {'col'}, dimensions={0}, use_global_device_ids=true | all-gather | bytes 491520 | tf_op jit(solution)/shard_map/all_gather | solution.py:44
  168.3 13.1 %fusion.10 = f32[64,3072]{1,0:T(8,128)} fusion(bf16[64,3072]{1,0:T(8,128)(2,1)S(1)} %all_gather.22, bf16[3072,3072]{1,0:T(8,128)(2,1)} %param.8), kind=kOutput, calls=%fused_computation.16 | convolution fusion | flops 1207959552 | bytes 20054016 | tf_op jit(solution)/shard_map/dot_general | solution.py:54
  181.5 0.0 reduce-scatter.14.cloned.1.call-update
  181.5 9.5 %convert_bitcast_fusion = bf16[3072,3072]{0,1:T(8,128)(2,1)} fusion(bf16[64,3072]{1,0:T(8,128)(2,1)S(1)} %all_gather.22, bf16[64,3072]{1,0:T(8,128)(2,1)S(1)} %all_gather.21), kind=kOutput, calls=%fused_computation | convolution fusion | flops 1217396736 | bytes 19660800 | tf_op jit(solution)/shard_map/dot_general | solution.py:49
  191.0 24.6 %copy.9 = bf16[3072,3072]{1,0:T(8,128)(2,1)} copy(bf16[3072,3072]{0,1:T(8,128)(2,1)} %convert_bitcast_fusion) | data formatting | bytes 37748736
  215.6 6.7 %all_gather.23 = bf16[64,3072]{1,0:T(8,128)(2,1)S(1)} all-gather(bf16[16,3072]{1,0:T(8,128)(2,1)S(1)} %get-tuple-element.8), channel_id=1, replica_groups=mesh['row'=8,'col'=4] {'col'}, dimensions={0}, use_global_device_ids=true | all-gather | bytes 491520 | tf_op jit(solution)/shard_map/all_gather | solution.py:43
  222.4 9.5 %convolution_convert_fusion = bf16[3072,3072]{1,0:T(8,128)(2,1)} fusion(bf16[64,3072]{1,0:T(8,128)(2,1)S(1)} %all_gather.23, bf16[64,3072]{1,0:T(8,128)(2,1)S(1)} %all_gather.20), kind=kOutput, calls=%fused_computation.1 | convolution fusion | flops 1217396736 | bytes 19660800 | tf_op jit(solution)/shard_map/dot_general | solution.py:46
  231.9 0.0 reduce-scatter.8.cloned.1.call-done
  231.9 1.5 convert_element_type.25
  233.4 59.5 %reduce-scatter.14.cloned.1.call-done = f32[8,3072]{1,0:T(8,128)} async-done(((f32[64,3072]{1,0:T(8,128)}), f32[8,3072]{1,0:T(8,128)}) %reduce-scatter.14.cloned.1.call-update) | async-done | bytes 98320 | tf_op jit(solution)/shard_map/reduce_scatter | solution.py:53
  292.9 1.5 convert_element_type.27
Async XLA Ops:
  7.2 43.8 %copy-start = (bf16[8,3072]{1,0:T(8,128)(2,1)S(1)}, bf16[8,3072]{1,0:T(8,128)(2,1)}, u32[]{:S(2)}) copy-start(bf16[8,3072]{1,0:T(8,128)(2,1)} %param.7) | copy-start | bytes 147460
  7.2 129.6 %reduce-scatter.6.cloned.1.call-start = ((), (), s32[]{:S(2)}) async-start(), calls=%async_computation.5 | async-start | bytes 983040 | tf_op jit(solution)/shard_map/reduce_scatter | solution.py:17
  40.2 54.8 %copy-start.1 = (bf16[8,3072]{1,0:T(8,128)(2,1)S(1)}, bf16[8,3072]{1,0:T(8,128)(2,1)}, u32[]{:S(2)}) copy-start(bf16[8,3072]{1,0:T(8,128)(2,1)} %param.6) | copy-start | bytes 147460
  50.9 104.4 %reduce-scatter.10.cloned.1.call-start = ((), (), s32[]{:S(2)}) async-start(), calls=%async_computation.7 | async-start | bytes 983040 | tf_op jit(solution)/shard_map/reduce_scatter | solution.py:37
  95.0 66.1 %reduce-scatter.12.cloned.1.call-start = ((), (), s32[]{:S(2)}) async-start(), calls=%async_computation.8 | async-start | bytes 983040 | tf_op jit(solution)/shard_map/reduce_scatter | solution.py:36
  136.7 95.2 %reduce-scatter.8.cloned.1.call-start = ((), (), s32[]{:S(2)}) async-start(), calls=%async_computation.6 | async-start | bytes 884736 | tf_op jit(solution)/shard_map/reduce_scatter | solution.py:21
  155.2 137.7 %reduce-scatter.14.cloned.1.call-start = ((), (), s32[]{:S(2)}) async-start(), calls=%async_computation.9 | async-start | bytes 884736 | tf_op jit(solution)/shard_map/reduce_scatter | solution.py:53
Sparse Core Ops, SparseCore 0:
  51.0 24.2 reduce-scatter.5
  95.1 24.2 reduce-scatter.9
  136.8 24.2 reduce-scatter.11
  164.2 63.2 reduce-scatter.7
  230.6 62.2 reduce-scatter.13
where the time goes:
time: 302 us; the launch traced here: 301 us
  blocking collectives  114 us (38%)
  matrix products  77.3 us (26%)
  waiting for transfers between devices  65.4 us (22%)
  local copies, waits for them, and re-layouts  24.6 us (8%)
  between operations  13.8 us (5%)
  other arithmetic  5.13 us (2%)
    reduce_scatter x1, waiting for transfers between devices, local(): lax.psum_scatter(lax.dot_general(block, w_in, (((1,), (1,)), ((), ())), p...  59.5 us
    all_gather x1, blocking collectives, local(): lax.all_gather(tokens, 'row', axis=0, tiled=True)  33 us
    all_gather x1, blocking collectives, local(): lax.all_gather(out_grad, 'row', axis=0, tiled=True)  31 us
    all_gather x1, blocking collectives, local(): lax.all_gather(past_tokens, 'row', axis=0, tiled=True)  31 us
    unnamed x5, local copies, waits for them, and re-layouts  24.6 us
    dot_general x1, matrix products, local(): lax.dot_general(block, w_in, (((1,), (1,)), ((), ())), preferred_element_...  13.1 us
    dot_general x1, matrix products, local(): lax.dot_general(grad_all, w_out, (((1,), (1,)), ((), ())), preferred_elem...  13.1 us
    dot_general x1, matrix products, local(): jnp.dot(block, w_out, preferred_element_type=jnp.float32)  10.8 us
  transfers between devices with their start and end apart: 5, of which 2 were waited for; matrix products, arithmetic and copies ran while one was open for 32% of the time, Pallas kernels for 0%

commit v1 on v0

--- a/solution.py
+++ b/solution.py
@@ -1,7 +1,42 @@
+import functools
 import jax
 import jax.numpy as jnp
 from jax import lax
 from jax.sharding import PartitionSpec as P
+
+
+def load_case_on(x_part, link_axis):
+    arr_out = lax.axis_index(link_axis)
+    local_out = lax.axis_size(link_axis)
+    parts_out, right_arr, block_now = (local_out, arr_out, x_part.shape[0])
+    newest = range(parts_out)
+    all_values = map(lambda j: (j, (j + 1) % parts_out), newest)
+    heap = list(all_values)
+    wide_out = range(parts_out)
+    arr_now = map(lambda j: (j, (j - 1) % parts_out), wide_out)
+    work_now = jnp.zeros(
+        (*x_part.shape[:0], parts_out * block_now, *x_part.shape[1:]), x_part.dtype
+    )
+    work_now = lax.dynamic_update_slice_in_dim(work_now, x_part, right_arr * block_now, axis=0)
+    arrivals = list(arr_now)
+    b_next = a_next = x_part
+    j0 = 1
+    outcome_arr = parts_out // 2
+    while j0 < outcome_arr + 1:
+        b_next = lax.ppermute(b_next, link_axis, perm=heap)
+        work_now = lax.dynamic_update_slice_in_dim(
+            work_now, b_next, (right_arr - j0) % parts_out * block_now, axis=0
+        )
+        if j0 < parts_out - outcome_arr:
+            a_next = lax.ppermute(a_next, link_axis, arrivals)
+            work_now = lax.dynamic_update_slice_in_dim(
+                work_now, a_next, (right_arr + j0) % parts_out * block_now, axis=0
+            )
+        j0 += 1
+    return work_now
+
+
+create_the_turns = functools.partial(load_case_on, link_axis="row")
 
 
 def gelu_parts(pre):
@@ -11,9 +46,7 @@
 
 
 def local(tokens, past_tokens, out_grad, w_in, w_out):
-    pre_part = jnp.dot(
-        lax.all_gather(tokens, "row", axis=0, tiled=True), w_in, preferred_element_type=jnp.float32
-    )
+    pre_part = jnp.dot(create_the_turns(tokens), w_in, preferred_element_type=jnp.float32)
     pre_share = lax.psum_scatter(pre_part, "col", scatter_dimension=0, tiled=True)
     hidden_share = gelu_parts(pre_share)[0].astype(jnp.bfloat16)
     hidden_all = lax.all_gather(hidden_share, "col", axis=0, tiled=True)

time: 302 us -> 297 us (0.983)
  blocking collectives: 114 us -> 83.9 us
  starting transfers between devices: 0.21 us -> 14.4 us
  waiting for transfers between devices: 65.4 us -> 76.6 us
    reduce_scatter x1, waiting for transfers between devices: 0.01 us -> 61.2 us  [local(): lax.psum_scatter(jnp.dot(block, w_out, preferred_element_type=jnp.float32...]
    reduce_scatter x1, waiting for transfers between devices: 59.5 us -> 0.01 us  [local(): lax.psum_scatter(lax.dot_general(block, w_in, (((1,), (1,)), ((), ())), p...]
    all_gather x1 -> x0, blocking collectives: 33 us -> none  [local(): lax.all_gather(tokens, 'row', axis=0, tiled=True)]
    ppermute x0 -> x7, waiting for transfers between devices: none -> 15.2 us  [the longest x4 13.5 us: load_case_on(): b_next = lax.ppermute(b_next, link_axis, perm=heap)]
    ppermute x0 -> x7, starting transfers between devices: none -> 14.2 us  [the longest x3 14.2 us: load_case_on(): a_next = lax.ppermute(a_next, link_axis, arrivals)]
    reduce_scatter x1, waiting for transfers between devices: 5.76 us -> 0.02 us  [local(): lax.psum_scatter(past_part, 'col', scatter_dimension=0, tiled=True)]
  transfers between devices with their start and end apart: 5 -> 12, of which waited for: 2 -> 4; matrix products, arithmetic and copies ran while one was open for 32% -> 31% of each run, Pallas kernels for 0% -> 0%
where the time goes in v1:
time: 297 us; the launch traced here: 296 us
  blocking collectives  83.9 us (28%)
  matrix products  77.3 us (26%)
  waiting for transfers between devices  76.6 us (26%)
  local copies, waits for them, and re-layouts  24.7 us (8%)
  starting transfers between devices  14.4 us (5%)
  between operations  14 us (5%)
  other arithmetic  5.13 us (2%)
    reduce_scatter x1, waiting for transfers between devices, local(): lax.psum_scatter(jnp.dot(block, w_out, preferred_element_type=jnp.float32...  61.2 us
    all_gather x1, blocking collectives, local(): lax.all_gather(out_grad, 'row', axis=0, tiled=True)  33 us
    all_gather x1, blocking collectives, local(): lax.all_gather(past_tokens, 'row', axis=0, tiled=True)  31 us
    unnamed x5, local copies, waits for them, and re-layouts  24.6 us
    ppermute x3, starting transfers between devices, load_case_on(): a_next = lax.ppermute(a_next, link_axis, arrivals)  14.2 us
    ppermute x4, waiting for transfers between devices, load_case_on(): b_next = lax.ppermute(b_next, link_axis, perm=heap)  13.5 us
    dot_general x1, matrix products, local(): lax.dot_general(block, w_in, (((1,), (1,)), ((), ())), preferred_element_...  13.2 us
    dot_general x1, matrix products, local(): lax.dot_general(grad_all, w_out, (((1,), (1,)), ((), ())), preferred_elem...  13.1 us
  transfers between devices with their start and end apart: 12, of which 4 were waited for; matrix products, arithmetic and copies ran while one was open for 31% of the time, Pallas kernels for 0%

profile of v1, /device:TPU:0, one launch (start us, length us, event | category | flops | bytes accessed | tf_op | source)
XLA Modules:
  0.0 296.1 jit_solution(5172029676531698970)
XLA Ops:
  7.2 0.0 copy-start.1
  7.2 0.0 copy-start
  7.2 0.0 reduce-scatter.10.cloned.1.call-start
  7.2 33.0 %all_gather.16 = bf16[64,3072]{1,0:T(8,128)(2,1)S(1)} all-gather(bf16[8,3072]{1,0:T(8,128)(2,1)} %param.7), channel_id=1, replica_groups=mesh['row'=8,'col'=4] {'row'}, dimensions={0}, use_global_device_ids=true | all-gather | bytes 442368 | tf_op jit(solution)/shard_map/all_gather | solution.py:62
  40.2 13.1 %fusion.8 = f32[64,3072]{1,0:T(8,128)} fusion(bf16[64,3072]{1,0:T(8,128)(2,1)S(1)} %all_gather.16, bf16[3072,3072]{1,0:T(8,128)(2,1)} %param.9), kind=kOutput, calls=%fused_computation.22 | convolution fusion | flops 1207959552 | bytes 20054016 | tf_op jit(solution)/shard_map/dot_general | solution.py:65
  53.3 0.0 reduce-scatter.10.cloned.1.call-update
  53.3 0.0 reduce-scatter.12.cloned.1.call-start
  53.3 0.0 copy-done.1
  53.4 4.4 %collective-permute-start.1 = (bf16[8,3072]{1,0:T(8,128)(2,1)S(1)}, bf16[8,3072]{1,0:T(8,128)(2,1)S(1)}, u32[]{:S(2)}, u32[]{:S(2)}) collective-permute-start(bf16[8,3072]{1,0:T(8,128)(2,1)S(1)} %copy-done.1), channel_id=1, source_target_pairs={{0,28},{4,0},{8,4},{12,8},{16,12},{20,16},{24,20},{28,24},{1,29},{... | collective-permute-start | bytes 147464 | tf_op jit(solution)/shard_map/ppermute | solution.py:31
  57.7 0.0 collective-permute-start
  57.7 31.0 %all_gather.17 = bf16[64,3072]{1,0:T(8,128)(2,1)S(1)} all-gather(bf16[8,3072]{1,0:T(8,128)(2,1)S(1)} %copy-done), channel_id=1, replica_groups=mesh['row'=8,'col'=4] {'row'}, dimensions={0}, use_global_device_ids=true | all-gather | bytes 442368 | tf_op jit(solution)/shard_map/all_gather | solution.py:61
  88.7 10.6 %fusion.9 = f32[64,3072]{1,0:T(8,128)} fusion(bf16[64,3072]{1,0:T(8,128)(2,1)S(1)} %all_gather.17, bf16[3072,3072]{1,0:T(8,128)(2,1)} %param.8), kind=kOutput, calls=%fused_computation.23 | convolution fusion | flops 1207959552 | bytes 20054016 | tf_op jit(solution)/shard_map/dot_general | solution.py:64
  99.3 0.0 reduce-scatter.12.cloned.1.call-update
  99.3 0.0 reduce-scatter.6.cloned.1.call-start
  99.6 0.0 collective-permute-done.1
  99.6 4.8 %collective-permute-start.3 = (bf16[8,3072]{1,0:T(8,128)(2,1)S(1)}, bf16[8,3072]{1,0:T(8,128)(2,1)S(1)}, u32[]{:S(2)}, u32[]{:S(2)}) collective-permute-start(bf16[8,3072]{1,0:T(8,128)(2,1)S(1)} %collective-permute-done.1), channel_id=1, source_target_pairs={{0,28},{4,0},{8,4},{12,8},{16,12},{20,16},{24,20},{28,24},{1,29},{... | collective-permute-start | bytes 147464 | tf_op jit(solution)/shard_map/ppermute | solution.py:31
  104.4 0.0 collective-permute-done
  104.4 0.0 collective-permute-start.2
  104.4 1.7 collective-permute-done.3
  106.1 5.0 %collective-permute-start.5 = (bf16[8,3072]{1,0:T(8,128)(2,1)S(1)}, bf16[8,3072]{1,0:T(8,128)(2,1)S(1)}, u32[]{:S(2)}, u32[]{:S(2)}) collective-permute-start(bf16[8,3072]{1,0:T(8,128)(2,1)S(1)} %collective-permute-done.3), channel_id=1, source_target_pairs={{0,28},{4,0},{8,4},{12,8},{16,12},{20,16},{24,20},{28,24},{1,29},{... | collective-permute-start | bytes 147464 | tf_op jit(solution)/shard_map/ppermute | solution.py:31
  111.2 0.0 collective-permute-done.2
  111.2 0.0 collective-permute-start.4
  111.2 6.8 %collective-permute-done.4 = bf16[8,3072]{1,0:T(8,128)(2,1)S(1)} collective-permute-done((bf16[8,3072]{1,0:T(8,128)(2,1)S(1)}, bf16[8,3072]{1,0:T(8,128)(2,1)S(1)}, u32[]{:S(2)}, u32[]{:S(2)}) %collective-permute-start.4) | collective-permute-done | bytes 49184 | tf_op jit(solution)/shard_map/ppermute | solution.py:26
  117.9 0.0 collective-permute-start.6
  118.0 0.0 collective-permute-done.5
  118.0 6.7 %collective-permute-done.6 = bf16[8,3072]{1,0:T(8,128)(2,1)S(1)} collective-permute-done((bf16[8,3072]{1,0:T(8,128)(2,1)S(1)}, bf16[8,3072]{1,0:T(8,128)(2,1)S(1)}, u32[]{:S(2)}, u32[]{:S(2)}) %collective-permute-start.6) | collective-permute-done | bytes 49184 | tf_op jit(solution)/shard_map/ppermute | solution.py:26
  124.7 10.6 %fusion.6 = f32[64,3072]{1,0:T(8,128)} fusion(bf16[64,3072]{1,0:T(8,128)(2,1)S(1)} %constant_dynamic-update-slice_fusion, bf16[3072,3072]{1,0:T(8,128)(2,1)} %param.8), kind=kOutput, calls=%fused_computation.20 | convolution fusion | flops 1207959552 | bytes 20054016 | tf_op jit(solution)/shard_map/dot_general | solution.py:49
  135.4 0.0 reduce-scatter.6.cloned.1.call-update
  135.4 0.0 reduce-scatter.14.cloned.1.call-start
  135.4 0.0 reduce-scatter.10.cloned.1.call-done
  135.5 0.0 reduce-scatter.12.cloned.1.call-done
  135.5 1.1 multiply_convert_fusion
  136.6 6.7 %all_gather.18 = bf16[64,3072]{1,0:T(8,128)(2,1)S(1)} all-gather(bf16[16,3072]{1,0:T(8,128)(2,1)S(1)} %get-tuple-element.9), channel_id=1, replica_groups=mesh['row'=8,'col'=4] {'col'}, dimensions={0}, use_global_device_ids=true | all-gather | bytes 491520 | tf_op jit(solution)/shard_map/all_gather | solution.py:77
  143.3 13.2 %fusion.10 = f32[64,3072]{1,0:T(8,128)} fusion(bf16[64,3072]{1,0:T(8,128)(2,1)S(1)} %all_gather.18, bf16[3072,3072]{1,0:T(8,128)(2,1)} %param.8), kind=kOutput, calls=%fused_computation.24 | convolution fusion | flops 1207959552 | bytes 20054016 | tf_op jit(solution)/shard_map/dot_general | solution.py:87
  156.5 0.0 reduce-scatter.14.cloned.1.call-update
  156.5 0.0 reduce-scatter.8.cloned.1.call-start
  156.5 0.0 reduce-scatter.6.cloned.1.call-done
  156.6 1.0 multiply_convert_fusion.1
  157.5 6.6 %all_gather.15 = bf16[64,3072]{1,0:T(8,128)(2,1)S(1)} all-gather(bf16[16,3072]{1,0:T(8,128)(2,1)S(1)} %multiply_convert_fusion.1), channel_id=1, replica_groups=mesh['row'=8,'col'=4] {'col'}, dimensions={0}, use_global_device_ids=true | all-gather | bytes 491520 | tf_op jit(solution)/shard_map/all_gather | solution.py:52
  164.1 10.8 %fusion.7 = f32[64,3072]{1,0:T(8,128)} fusion(bf16[64,3072]{1,0:T(8,128)(2,1)S(1)} %all_gather.15, bf16[3072,3072]{1,0:T(8,128)(2,1)} %param.9), kind=kOutput, calls=%fused_computation.21 | convolution fusion | flops 1207959552 | bytes 20054016 | tf_op jit(solution)/shard_map/dot_general | solution.py:55
  174.9 0.0 reduce-scatter.8.cloned.1.call-update
  174.9 9.5 %convert_bitcast_fusion = bf16[3072,3072]{0,1:T(8,128)(2,1)} fusion(bf16[64,3072]{1,0:T(8,128)(2,1)S(1)} %all_gather.18, bf16[64,3072]{1,0:T(8,128)(2,1)S(1)} %all_gather.17), kind=kOutput, calls=%fused_computation | convolution fusion | flops 1217396736 | bytes 19660800 | tf_op jit(solution)/shard_map/dot_general | solution.py:82
  184.4 24.6 %copy.9 = bf16[3072,3072]{1,0:T(8,128)(2,1)} copy(bf16[3072,3072]{0,1:T(8,128)(2,1)} %convert_bitcast_fusion) | data formatting | bytes 37748736
  209.0 6.8 %all_gather.19 = bf16[64,3072]{1,0:T(8,128)(2,1)S(1)} all-gather(bf16[16,3072]{1,0:T(8,128)(2,1)S(1)} %get-tuple-element.8), channel_id=1, replica_groups=mesh['row'=8,'col'=4] {'col'}, dimensions={0}, use_global_device_ids=true | all-gather | bytes 491520 | tf_op jit(solution)/shard_map/all_gather | solution.py:76
  215.8 9.5 %convolution_convert_fusion = bf16[3072,3072]{1,0:T(8,128)(2,1)} fusion(bf16[64,3072]{1,0:T(8,128)(2,1)S(1)} %all_gather.19, bf16[64,3072]{1,0:T(8,128)(2,1)S(1)} %all_gather.16), kind=kOutput, calls=%fused_computation.1 | convolution fusion | flops 1217396736 | bytes 19660800 | tf_op jit(solution)/shard_map/dot_general | solution.py:79
  225.3 1.5 convert_element_type.27
  226.8 61.2 %reduce-scatter.8.cloned.1.call-done = f32[8,3072]{1,0:T(8,128)} async-done(((f32[64,3072]{1,0:T(8,128)}), f32[8,3072]{1,0:T(8,128)}) %reduce-scatter.8.cloned.1.call-update) | async-done | bytes 98320 | tf_op jit(solution)/shard_map/reduce_scatter | solution.py:54
  288.1 1.5 convert_element_type.25
  (11 shorter events, 0.1 us)
Async XLA Ops:
  7.2 46.2 %copy-start.1 = (bf16[8,3072]{1,0:T(8,128)(2,1)S(1)}, bf16[8,3072]{1,0:T(8,128)(2,1)}, u32[]{:S(2)}) copy-start(bf16[8,3072]{1,0:T(8,128)(2,1)} %param.5) | copy-start | bytes 147460
  7.2 50.6 %copy-start = (bf16[8,3072]{1,0:T(8,128)(2,1)S(1)}, bf16[8,3072]{1,0:T(8,128)(2,1)}, u32[]{:S(2)}) copy-start(bf16[8,3072]{1,0:T(8,128)(2,1)} %param.6) | copy-start | bytes 147460
  7.2 128.3 %reduce-scatter.10.cloned.1.call-start = ((), (), s32[]{:S(2)}) async-start(), calls=%async_computation.7 | async-start | bytes 983040 | tf_op jit(solution)/shard_map/reduce_scatter | solution.py:70
  53.3 82.2 %reduce-scatter.12.cloned.1.call-start = ((), (), s32[]{:S(2)}) async-start(), calls=%async_computation.8 | async-start | bytes 983040 | tf_op jit(solution)/shard_map/reduce_scatter | solution.py:69
  53.4 46.2 %collective-permute-start.1 = (bf16[8,3072]{1,0:T(8,128)(2,1)S(1)}, bf16[8,3072]{1,0:T(8,128)(2,1)S(1)}, u32[]{:S(2)}, u32[]{:S(2)}) collective-permute-start(bf16[8,3072]{1,0:T(8,128)(2,1)S(1)} %copy-done.1), channel_id=1, source_target_pairs={{0,28},{4,0},{8,4},{12,8},{16,12},{20,16},{24,20},{28,24},{1,29},{... | collective-permute-start | bytes 147464 | tf_op jit(solution)/shard_map/ppermute | solution.py:31
  57.7 46.6 %collective-permute-start = (bf16[8,3072]{1,0:T(8,128)(2,1)S(1)}, bf16[8,3072]{1,0:T(8,128)(2,1)S(1)}, u32[]{:S(2)}, u32[]{:S(2)}) collective-permute-start(bf16[8,3072]{1,0:T(8,128)(2,1)S(1)} %copy-done.1), channel_id=1, source_target_pairs={{0,4},{4,8},{8,12},{12,16},{16,20},{20,24},{24,28},{28,0},{1,5},{5... | collective-permute-start | bytes 147464 | tf_op jit(solution)/shard_map/ppermute | solution.py:26
  99.3 57.2 %reduce-scatter.6.cloned.1.call-start = ((), (), s32[]{:S(2)}) async-start(), calls=%async_computation.5 | async-start | bytes 983040 | tf_op jit(solution)/shard_map/reduce_scatter | solution.py:50
  99.6 6.5 %collective-permute-start.3 = (bf16[8,3072]{1,0:T(8,128)(2,1)S(1)}, bf16[8,3072]{1,0:T(8,128)(2,1)S(1)}, u32[]{:S(2)}, u32[]{:S(2)}) collective-permute-start(bf16[8,3072]{1,0:T(8,128)(2,1)S(1)} %collective-permute-done.1), channel_id=1, source_target_pairs={{0,28},{4,0},{8,4},{12,8},{16,12},{20,16},{24,20},{28,24},{1,29},{... | collective-permute-start | bytes 147464 | tf_op jit(solution)/shard_map/ppermute | solution.py:31
  104.4 6.8 %collective-permute-start.2 = (bf16[8,3072]{1,0:T(8,128)(2,1)S(1)}, bf16[8,3072]{1,0:T(8,128)(2,1)S(1)}, u32[]{:S(2)}, u32[]{:S(2)}) collective-permute-start(bf16[8,3072]{1,0:T(8,128)(2,1)S(1)} %collective-permute-done), channel_id=1, source_target_pairs={{0,4},{4,8},{8,12},{12,16},{16,20},{20,24},{24,28},{28,0},{1,5},{5... | collective-permute-start | bytes 147464 | tf_op jit(solution)/shard_map/ppermute | solution.py:26
  106.1 11.8 %collective-permute-start.5 = (bf16[8,3072]{1,0:T(8,128)(2,1)S(1)}, bf16[8,3072]{1,0:T(8,128)(2,1)S(1)}, u32[]{:S(2)}, u32[]{:S(2)}) collective-permute-start(bf16[8,3072]{1,0:T(8,128)(2,1)S(1)} %collective-permute-done.3), channel_id=1, source_target_pairs={{0,28},{4,0},{8,4},{12,8},{16,12},{20,16},{24,20},{28,24},{1,29},{... | collective-permute-start | bytes 147464 | tf_op jit(solution)/shard_map/ppermute | solution.py:31
  111.2 6.8 %collective-permute-start.4 = (bf16[8,3072]{1,0:T(8,128)(2,1)S(1)}, bf16[8,3072]{1,0:T(8,128)(2,1)S(1)}, u32[]{:S(2)}, u32[]{:S(2)}) collective-permute-start(bf16[8,3072]{1,0:T(8,128)(2,1)S(1)} %collective-permute-done.2), channel_id=1, source_target_pairs={{0,4},{4,8},{8,12},{12,16},{16,20},{20,24},{24,28},{28,0},{1,5},{5... | collective-permute-start | bytes 147464 | tf_op jit(solution)/shard_map/ppermute | solution.py:26
  117.9 6.8 %collective-permute-start.6 = (bf16[8,3072]{1,0:T(8,128)(2,1)S(1)}, bf16[8,3072]{1,0:T(8,128)(2,1)S(1)}, u32[]{:S(2)}, u32[]{:S(2)}) collective-permute-start(bf16[8,3072]{1,0:T(8,128)(2,1)S(1)} %collective-permute-done.4), channel_id=1, source_target_pairs={{0,4},{4,8},{8,12},{12,16},{16,20},{20,24},{24,28},{28,0},{1,5},{5... | collective-permute-start | bytes 147464 | tf_op jit(solution)/shard_map/ppermute | solution.py:26
  135.4 89.9 %reduce-scatter.14.cloned.1.call-start = ((), (), s32[]{:S(2)}) async-start(), calls=%async_computation.9 | async-start | bytes 884736 | tf_op jit(solution)/shard_map/reduce_scatter | solution.py:86
  156.5 131.6 %reduce-scatter.8.cloned.1.call-start = ((), (), s32[]{:S(2)}) async-start(), calls=%async_computation.6 | async-start | bytes 884736 | tf_op jit(solution)/shard_map/reduce_scatter | solution.py:54
Sparse Core Ops, SparseCore 0:
  53.4 24.2 reduce-scatter.9
  99.5 24.6 reduce-scatter.11
  135.5 20.5 reduce-scatter.5
  159.2 63.2 reduce-scatter.13
  225.7 62.3 reduce-scatter.7
